TPU v7x, 32 devices: a whole 2x2x4 slice. The times are simulated.
32 devices in a mesh: section: 2 (over x), dp: 8 (over z, y), mp: 2 (over core).
Axes of the slice: x: 2, y: 2, z: 4, core: 2. Of those that a mesh axis runs over, the one named last changes fastest.
Arguments:
- layer_inputs: bfloat16 [2, 128, 4096], P('section', None, 'mp'), may hold values from -6 to 6
- pre_act: bfloat16 [2, 128, 8192], P('section', None, 'dp'), may hold values from -6 to 6
- out_grad: bfloat16 [128, 4096], P(None, 'mp'), may hold values from -4 to 4
- w_in: bfloat16 [8, 2, 512, 4096], P('dp', 'section', None, 'mp'), may hold values from -0.09375 to 0.09375
- w_out: bfloat16 [8, 2, 512, 4096], P('dp', 'section', None, 'mp'), may hold values from -0.0625 to 0.0625
Outputs:
- in_grads: bfloat16 [2, 128, 4096], P('section', None, 'mp')
- grad_in: float32 [8, 2, 512, 4096], P('dp', 'section', None, 'mp')
- grad_out: float32 [8, 2, 512, 4096], P('dp', 'section', None, 'mp')
All inputs are finite; a program needn't handle non-finite values.
Results may differ from a plain program's by a relative error of at most 0.035.
Values may be sent and summed in bfloat16 or wider, within the bound.
A program may use at most 64 MiB of HBM per device.

v0:
```python
import jax
import jax.numpy as jnp
from jax import lax
from jax.sharding import PartitionSpec as P

MICRO = 2


def shifted(value, axis, by):
    size = lax.axis_size(axis)
    pairs = [(i, i + by) for i in range(size) if 0 <= i + by < size]
    return lax.ppermute(value, axis, pairs)


def gelu_slope(value):
    cdf = 0.5 * (1.0 + lax.erf(value * 0.7071067811865476))
    dens = jnp.exp(-0.5 * value * value) * 0.3989422804014327
    return cdf + value * dens


def rounded(value):
    return lax.optimization_barrier(value.astype(jnp.bfloat16)).astype(jnp.float32)


def by_tokens(left, right):
    return lax.dot_general(
        left, right, (((0,), (0,)), ((), ())), preferred_element_type=jnp.float32
    )


def body(layer_inputs, pre_act, out_grad, w_in, w_out):
    sections = lax.axis_size("section")
    spot = lax.axis_index("section")
    tok_rows = out_grad.shape[0]
    block = tok_rows // MICRO
    width = out_grad.shape[1]
    full_in, full_out = (
        lax.all_gather(w_in, "section", axis=1, tiled=True),
        lax.all_gather(w_out, "section", axis=1, tiled=True),
    )
    units = full_in.shape[1] * full_in.shape[2]
    per_block = full_in.shape[2]
    in_rows = full_in.reshape(units, width)
    out_rows = full_out.reshape(units, width)
    inputs = layer_inputs[0]
    saved = pre_act[0]
    is_last = spot == sections - 1

    def advance(step, state):
        incoming, dys, gees, results = state
        micro_id = step - (sections - 1 - spot)
        valid = jnp.logical_and(micro_id >= 0, micro_id < MICRO)
        begin = jnp.clip(micro_id, 0, MICRO - 1) * block
        given = lax.dynamic_slice_in_dim(out_grad, begin, block, 0)
        upper = jnp.where(is_last, given, incoming)
        partial_value = lax.dot_general(
            upper, out_rows, (((1,), (1,)), ((), ())), preferred_element_type=jnp.float32
        )
        summed = lax.psum(partial_value.astype(jnp.bfloat16), "mp").astype(jnp.float32)
        rows_pre = lax.dynamic_slice_in_dim(saved, begin, block, 0).astype(jnp.float32)
        gee = (summed * gelu_slope(rows_pre)).astype(jnp.bfloat16)
        branch = jnp.dot(gee, in_rows, preferred_element_type=jnp.float32)
        total = lax.psum(branch.astype(jnp.bfloat16), "dp").astype(jnp.float32)
        result = (upper.astype(jnp.float32) + total).astype(jnp.bfloat16)
        outgoing = shifted(result, "section", -1)
        old_dy = lax.dynamic_slice_in_dim(dys, begin, block, 0)
        old_gee = lax.dynamic_slice_in_dim(gees, begin, block, 0)
        old_res = lax.dynamic_slice_in_dim(results, begin, block, 0)
        dys = lax.dynamic_update_slice_in_dim(dys, jnp.where(valid, upper, old_dy), begin, 0)
        gees = lax.dynamic_update_slice_in_dim(gees, jnp.where(valid, gee, old_gee), begin, 0)
        results = lax.dynamic_update_slice_in_dim(
            results, jnp.where(valid, result, old_res), begin, 0
        )
        return (outgoing, dys, gees, results)

    start_state = (
        jnp.zeros((block, width), jnp.bfloat16),
        jnp.zeros((tok_rows, width), jnp.bfloat16),
        jnp.zeros((tok_rows, units), jnp.bfloat16),
        jnp.zeros((tok_rows, width), jnp.bfloat16),
    )
    final_state = lax.fori_loop(0, sections + MICRO - 1, advance, start_state)
    dys = final_state[1]
    gees = final_state[2]
    results = final_state[3]
    hidden = jax.nn.gelu(saved.astype(jnp.float32), approximate=False).astype(jnp.bfloat16)
    offset = spot * per_block
    empty = jnp.zeros((per_block, width), jnp.float32)
    piece = (
        lax.all_gather(inputs[None], "section", axis=0, tiled=True),
        lax.all_gather(dys[None], "section", axis=0, tiled=True),
        lax.all_gather(gees[None], "section", axis=0, tiled=True),
        lax.all_gather(hidden[None], "section", axis=0, tiled=True),
    )
    acc_in = empty
    acc_out = empty
    for row in range(piece[0].shape[0]):
        gee_cols = lax.dynamic_slice_in_dim(piece[2][row], offset, per_block, 1)
        hid_cols = lax.dynamic_slice_in_dim(piece[3][row], offset, per_block, 1)
        acc_in = acc_in + rounded(by_tokens(gee_cols, piece[0][row]))
        acc_out = acc_out + rounded(by_tokens(hid_cols, piece[1][row]))
    acc_in, acc_out = (acc_in, acc_out)
    grad_in = acc_in.reshape(1, 1, per_block, width)
    grad_out = acc_out.reshape(1, 1, per_block, width)
    return (results[None], grad_in, grad_out)


def solution(mesh):
    in_specs = (
        P("section", None, "mp"),
        P("section", None, "dp"),
        P(None, "mp"),
        P("dp", "section", None, "mp"),
        P("dp", "section", None, "mp"),
    )
    out_specs = (
        P("section", None, "mp"),
        P("dp", "section", None, "mp"),
        P("dp", "section", None, "mp"),
    )
    return jax.shard_map(body, mesh=mesh, in_specs=in_specs, out_specs=out_specs, check_vma=False)
```

profile of v0, /device:TPU:0, one launch (start us, length us, event | category | flops | bytes accessed | tf_op | source)
XLA Modules:
  0.0 509.6 jit_solution(17135875296356808804)
XLA Ops:
  8.7 60.3 %all-gather.7.cloned.1.call-done = bf16[1,2,512,2048]{3,2,0,1:T(8,128)(2,1)} async-done(((bf16[1,1,512,2048]{3,2,0,1:T(8,128)(2,1)}), bf16[1,2,512,2048]{3,2,0,1:T(8,128)(2,1)}) %all-gather.7.cloned.1.call-update) | async-done | bytes 4194320 | tf_op jit(solution)/shard_map/all_gather | solution.py:39
  69.0 58.3 %all-gather.9.cloned.1.call-done = bf16[1,2,512,2048]{3,2,0,1:T(8,128)(2,1)} async-done(((bf16[1,1,512,2048]{3,2,0,1:T(8,128)(2,1)}), bf16[1,2,512,2048]{3,2,0,1:T(8,128)(2,1)}) %all-gather.9.cloned.1.call-update) | async-done | bytes 4194320 | tf_op jit(solution)/shard_map/all_gather | solution.py:38
  127.5 320.8 %while.21 = (s32[]{:T(128)}, bf16[64,2048]{1,0:T(8,128)(2,1)S(1)}, bf16[128,2048]{1,0:T(8,128)(2,1)S(1)}, bf16[128,1024]{1,0:T(8,128)(2,1)S(1)}, bf16[128,2048]{...) while((s32[]{:T(128)}, bf16[64,2048]{1,0:T(8,128)(2,1)S(1)}, ...), condition=%wide.region_3.4_spmd, body=%wide.region_0.3_spmd.sunk | while | flops 539820032 | bytes 16384420 | solution.py:82
  127.7 4.2 convolution_convert_fusion.8
  132.0 18.0 %all-reduce.3.cloned.1.call-done = bf16[64,1024]{1,0:T(8,128)(2,1)} async-done(((bf16[64,1024]{1,0:T(8,128)(2,1)}), bf16[64,1024]{1,0:T(8,128)(2,1)}) %all-reduce.3.cloned.1.call-update) | async-done | bytes 131088 | tf_op jit(solution)/shard_map/while/body/eval_jaxpr/psum | solution.py:59
  150.0 3.9 convolution_convert_fusion.9
  153.9 72.4 %all-reduce.5.cloned.1.call-done = bf16[64,2048]{1,0:T(8,128)(2,1)} async-done(((bf16[64,2048]{1,0:T(8,128)(2,1)}), bf16[64,2048]{1,0:T(8,128)(2,1)}) %all-reduce.5.cloned.1.call-update) | async-done | bytes 262160 | tf_op jit(solution)/shard_map/while/body/eval_jaxpr/psum | solution.py:63
  227.3 1.3 collective-permute-start
  228.8 6.8 %collective-permute-done = bf16[64,2048]{1,0:T(8,128)(2,1)S(1)} collective-permute-done((bf16[64,2048]{1,0:T(8,128)(2,1)S(1)}, bf16[64,2048]{1,0:T(8,128)(2,1)S(1)}, u32[]{:S(2)}, u32[]{:S(2)}) %collective-permute-start) | collective-permute-done | bytes 262176 | tf_op jit(solution)/shard_map/while/body/eval_jaxpr/ppermute | solution.py:12
  235.7 4.2 convolution_convert_fusion.8
  240.1 16.3 %all-reduce.3.cloned.1.call-done = bf16[64,1024]{1,0:T(8,128)(2,1)} async-done(((bf16[64,1024]{1,0:T(8,128)(2,1)}), bf16[64,1024]{1,0:T(8,128)(2,1)}) %all-reduce.3.cloned.1.call-update) | async-done | bytes 131088 | tf_op jit(solution)/shard_map/while/body/eval_jaxpr/psum | solution.py:59
  256.4 3.9 convolution_convert_fusion.9
  260.3 72.4 %all-reduce.5.cloned.1.call-done = bf16[64,2048]{1,0:T(8,128)(2,1)} async-done(((bf16[64,2048]{1,0:T(8,128)(2,1)}), bf16[64,2048]{1,0:T(8,128)(2,1)}) %all-reduce.5.cloned.1.call-update) | async-done | bytes 262160 | tf_op jit(solution)/shard_map/while/body/eval_jaxpr/psum | solution.py:63
  333.7 1.3 collective-permute-start
  335.2 6.8 %collective-permute-done = bf16[64,2048]{1,0:T(8,128)(2,1)S(1)} collective-permute-done((bf16[64,2048]{1,0:T(8,128)(2,1)S(1)}, bf16[64,2048]{1,0:T(8,128)(2,1)S(1)}, u32[]{:S(2)}, u32[]{:S(2)}) %collective-permute-start) | collective-permute-done | bytes 262176 | tf_op jit(solution)/shard_map/while/body/eval_jaxpr/ppermute | solution.py:12
  342.1 4.2 convolution_convert_fusion.8
  346.4 16.3 %all-reduce.3.cloned.1.call-done = bf16[64,1024]{1,0:T(8,128)(2,1)} async-done(((bf16[64,1024]{1,0:T(8,128)(2,1)}), bf16[64,1024]{1,0:T(8,128)(2,1)}) %all-reduce.3.cloned.1.call-update) | async-done | bytes 131088 | tf_op jit(solution)/shard_map/while/body/eval_jaxpr/psum | solution.py:59
  362.7 3.9 convolution_convert_fusion.9
  366.6 72.4 %all-reduce.5.cloned.1.call-done = bf16[64,2048]{1,0:T(8,128)(2,1)} async-done(((bf16[64,2048]{1,0:T(8,128)(2,1)}), bf16[64,2048]{1,0:T(8,128)(2,1)}) %all-reduce.5.cloned.1.call-update) | async-done | bytes 262160 | tf_op jit(solution)/shard_map/while/body/eval_jaxpr/psum | solution.py:63
  440.1 1.3 collective-permute-start
  441.5 6.8 %collective-permute-done = bf16[64,2048]{1,0:T(8,128)(2,1)S(1)} collective-permute-done((bf16[64,2048]{1,0:T(8,128)(2,1)S(1)}, bf16[64,2048]{1,0:T(8,128)(2,1)S(1)}, u32[]{:S(2)}, u32[]{:S(2)}) %collective-permute-start) | collective-permute-done | bytes 262176 | tf_op jit(solution)/shard_map/while/body/eval_jaxpr/ppermute | solution.py:12
  449.1 1.1 fusion.10
  450.2 8.1 %all_gather.22 = bf16[2,128,1024]{2,1,0:T(8,128)(2,1)S(1)} all-gather(bf16[1,128,1024]{2,1,0:T(8,128)(2,1)S(1)} %fusion.10), channel_id=1, replica_groups=mesh['section'=2,'dp'=8,'mp'=2] {'section'}, dimensions={0}, use_global_device_ids=true | all-gather | bytes 786432 | tf_op jit(solution)/shard_map/all_gather | solution.py:93
  458.3 12.7 %all-gather = bf16[256,1024]{1,0:T(8,128)(2,1)S(1)} all-gather(bf16[128,1024]{1,0:T(8,128)(2,1)S(1)} %get-tuple-element.260), channel_id=2, replica_groups=mesh['section'=2,'dp'=8,'mp'=2] {'section'}, dimensions={0}, use_global_device_ids=true | all-gather | bytes 786432 | tf_op jit(solution)/shard_map/all_gather | solution.py:92
  471.1 3.3 all-gather.11.cloned.1.call-done
  474.4 1.8 convolution_convert_fusion.4
  476.2 1.8 convolution_convert_fusion.5
  478.0 2.8 add_bitcast_fusion.1
  480.8 15.6 %all-gather.13.cloned.1.call-done = bf16[256,2048]{1,0:T(8,128)(2,1)} async-done(((bf16[128,2048]{1,0:T(8,128)(2,1)}), bf16[256,2048]{1,0:T(8,128)(2,1)}) %all-gather.13.cloned.1.call-update) | async-done | bytes 1048592 | tf_op jit(solution)/shard_map/all_gather | solution.py:91
  496.4 1.8 convolution_convert_fusion.2
  498.1 1.8 convolution_convert_fusion.3
  499.9 2.8 add_bitcast_fusion
  (49 shorter events, 6.7 us)
Async XLA Ops:
  7.2 120.3 %copy-start.4 = (bf16[128,2048]{1,0:T(8,128)(2,1)S(1)}, bf16[128,2048]{1,0:T(8,128)(2,1)}, u32[]{:S(2)}) copy-start(bf16[128,2048]{1,0:T(8,128)(2,1)} %param.9) | copy-start | bytes 1572868
  7.2 120.3 %copy-start.2 = (bf16[1,128,1024]{2,1,0:T(8,128)(2,1)S(1)}, bf16[1,128,1024]{2,1,0:T(8,128)(2,1)}, u32[]{:S(2)}) copy-start(bf16[1,128,1024]{2,1,0:T(8,128)(2,1)} %param.8) | copy-start | bytes 786436
  7.2 61.8 %all-gather.7.cloned.1.call-start = ((), (), s32[]{:S(2)}) async-start(), calls=%async_computation | async-start | bytes 6291456 | tf_op jit(solution)/shard_map/all_gather | solution.py:39
  7.9 119.4 %all-gather.9.cloned.1.call-start = ((), (), s32[]{:S(2)}) async-start(), calls=%async_computation.1 | async-start | bytes 6291456 | tf_op jit(solution)/shard_map/all_gather | solution.py:38
  127.5 22.5 %all-reduce.3.cloned.1.call-start = ((), (), s32[]{:S(2)}) async-start(), calls=%async_computation.4 | async-start | bytes 262144 | tf_op jit(solution)/shard_map/while/body/eval_jaxpr/psum | solution.py:59
  132.0 94.3 %all-reduce.5.cloned.1.call-start = ((), (), s32[]{:S(2)}) async-start(), calls=%async_computation.5 | async-start | bytes 524288 | tf_op jit(solution)/shard_map/while/body/eval_jaxpr/psum | solution.py:63
  150.0 78.6 %copy-start = (bf16[64,1024]{1,0:T(8,128)(2,1)S(1)}, bf16[64,1024]{1,0:T(8,128)(2,1)}, u32[]{:S(2)}) copy-start(bf16[64,1024]{1,0:T(8,128)(2,1)} %all-reduce.3.cloned.1.call-done) | copy-start | bytes 393220 | tf_op jit(solution)/shard_map/while
  227.3 8.3 %collective-permute-start = (bf16[64,2048]{1,0:T(8,128)(2,1)S(1)}, bf16[64,2048]{1,0:T(8,128)(2,1)S(1)}, u32[]{:S(2)}, u32[]{:S(2)}) collective-permute-start(bf16[64,2048]{1,0:T(8,128)(2,1)S(1)} %get-tuple-element.364), channel_id=1, source_target_pairs={{16,0},{17,1},{18,2},{19,3},{20,4},{21,5},{22,6},{23,7},{24,8},{25... | collective-permute-start | bytes 786440 | tf_op jit(solution)/shard_map/while/body/eval_jaxpr/ppermute | solution.py:12
  235.6 20.8 %all-reduce.3.cloned.1.call-start = ((), (), s32[]{:S(2)}) async-start(), calls=%async_computation.4 | async-start | bytes 262144 | tf_op jit(solution)/shard_map/while/body/eval_jaxpr/psum | solution.py:59
  240.0 92.6 %all-reduce.5.cloned.1.call-start = ((), (), s32[]{:S(2)}) async-start(), calls=%async_computation.5 | async-start | bytes 524288 | tf_op jit(solution)/shard_map/while/body/eval_jaxpr/psum | solution.py:63
  256.4 78.6 %copy-start = (bf16[64,1024]{1,0:T(8,128)(2,1)S(1)}, bf16[64,1024]{1,0:T(8,128)(2,1)}, u32[]{:S(2)}) copy-start(bf16[64,1024]{1,0:T(8,128)(2,1)} %all-reduce.3.cloned.1.call-done) | copy-start | bytes 393220 | tf_op jit(solution)/shard_map/while
  333.7 8.3 %collective-permute-start = (bf16[64,2048]{1,0:T(8,128)(2,1)S(1)}, bf16[64,2048]{1,0:T(8,128)(2,1)S(1)}, u32[]{:S(2)}, u32[]{:S(2)}) collective-permute-start(bf16[64,2048]{1,0:T(8,128)(2,1)S(1)} %get-tuple-element.364), channel_id=1, source_target_pairs={{16,0},{17,1},{18,2},{19,3},{20,4},{21,5},{22,6},{23,7},{24,8},{25... | collective-permute-start | bytes 786440 | tf_op jit(solution)/shard_map/while/body/eval_jaxpr/ppermute | solution.py:12
  342.0 20.8 %all-reduce.3.cloned.1.call-start = ((), (), s32[]{:S(2)}) async-start(), calls=%async_computation.4 | async-start | bytes 262144 | tf_op jit(solution)/shard_map/while/body/eval_jaxpr/psum | solution.py:59
  346.4 92.6 %all-reduce.5.cloned.1.call-start = ((), (), s32[]{:S(2)}) async-start(), calls=%async_computation.5 | async-start | bytes 524288 | tf_op jit(solution)/shard_map/while/body/eval_jaxpr/psum | solution.py:63
  362.7 78.6 %copy-start = (bf16[64,1024]{1,0:T(8,128)(2,1)S(1)}, bf16[64,1024]{1,0:T(8,128)(2,1)}, u32[]{:S(2)}) copy-start(bf16[64,1024]{1,0:T(8,128)(2,1)} %all-reduce.3.cloned.1.call-done) | copy-start | bytes 393220 | tf_op jit(solution)/shard_map/while
  440.1 8.3 %collective-permute-start = (bf16[64,2048]{1,0:T(8,128)(2,1)S(1)}, bf16[64,2048]{1,0:T(8,128)(2,1)S(1)}, u32[]{:S(2)}, u32[]{:S(2)}) collective-permute-start(bf16[64,2048]{1,0:T(8,128)(2,1)S(1)} %get-tuple-element.364), channel_id=1, source_target_pairs={{16,0},{17,1},{18,2},{19,3},{20,4},{21,5},{22,6},{23,7},{24,8},{25... | collective-permute-start | bytes 786440 | tf_op jit(solution)/shard_map/while/body/eval_jaxpr/ppermute | solution.py:12
  448.3 22.7 %copy-start.1 = (bf16[128,2048]{1,0:T(8,128)(2,1)}, bf16[128,2048]{1,0:T(8,128)(2,1)S(1)}, u32[]{:S(2)}) copy-start(bf16[128,2048]{1,0:T(8,128)(2,1)S(1)} %get-tuple-element.261) | copy-start | bytes 1572868
  448.3 29.6 %copy-start.3 = (bf16[128,2048]{1,0:T(8,128)(2,1)}, bf16[128,2048]{1,0:T(8,128)(2,1)S(1)}, u32[]{:S(2)}) copy-start(bf16[128,2048]{1,0:T(8,128)(2,1)S(1)} %get-tuple-element.259) | copy-start | bytes 1572868
  448.3 26.1 %all-gather.11.cloned.1.call-start = ((), (), s32[]{:S(2)}) async-start(), calls=%async_computation.2 | async-start | bytes 1572864 | tf_op jit(solution)/shard_map/all_gather | solution.py:90
  449.1 47.3 %all-gather.13.cloned.1.call-start = ((), (), s32[]{:S(2)}) async-start(), calls=%async_computation.3 | async-start | bytes 1572864 | tf_op jit(solution)/shard_map/all_gather | solution.py:91
Sparse Core Ops, SparseCore 0:
  9.5 59.4 all-gather.6
  70.6 56.7 all-gather.8
  132.1 17.8 all-reduce.2
  154.0 72.1 all-reduce.4
  240.1 16.1 all-reduce.2
  260.4 72.2 all-reduce.4
  346.5 16.1 all-reduce.2
  366.7 72.2 all-reduce.4
  450.7 23.6 all-gather.10
  476.4 19.9 all-gather.12
where the time goes:
time: 510 us
  waiting for transfers between devices  428 us (84%)
  matrix products  31.4 us (6%)
  blocking collectives  20.7 us (4%)
  between operations  14.2 us (3%)
  other arithmetic  10.8 us (2%)
    psum x3, waiting for transfers between devices, advance(): total = lax.psum(branch.astype(jnp.bfloat16), 'dp').astype(jnp.float32)  217 us
    all_gather x1, waiting for transfers between devices, body(): lax.all_gather(w_out, 'section', axis=1, tiled=True)  60.3 us
    all_gather x1, waiting for transfers between devices, body(): lax.all_gather(w_in, 'section', axis=1, tiled=True)  58.3 us
    psum x3, waiting for transfers between devices, advance(): lax.psum(partial_value.astype(jnp.bfloat16), 'mp').astype(jnp.float32)  50.6 us
    ppermute x3, waiting for transfers between devices, shifted(): return lax.ppermute(value, axis, pairs)  20.4 us
    all_gather x1, waiting for transfers between devices, body(): lax.all_gather(dys[None], 'section', axis=0, tiled=True)  15.6 us
    dot_general x3, matrix products, advance(): lax.dot_general(upper, out_rows, (((1,), (1,)), ((), ())), preferred_elem...  12.7 us
    all_gather x1, blocking collectives, body(): lax.all_gather(gees[None], 'section', axis=0, tiled=True)  12.7 us
  transfers between devices with their start and end apart: 13, of which 13 were waited for; matrix products, arithmetic and copies ran while one was open for 2% of the time, Pallas kernels for 0%

commit v1 on v0

v1 whole, which is shorter than its diff:
```python
import functools

import jax
import jax.numpy as jnp
from jax import lax
from jax.experimental import pallas as pl
from jax.experimental.pallas import tpu as pltpu
from jax.sharding import PartitionSpec as P

MESH = pl.DeviceIdType.MESH
CHUNKS = 2
PIECES = 8
LANES = 128
VMEM_BYTES = 60 * 1024 * 1024


def gelu_cdf(value):
    return 0.5 * (1.0 + lax.erf(value * 0.7071067811865476))


def slope_from(value, cdf):
    dens = jnp.exp(-0.5 * value * value) * 0.3989422804014327
    return cdf + value * dens


def rounded(value):
    return lax.optimization_barrier(value.astype(jnp.bfloat16)).astype(jnp.float32)


def by_tokens(left, right):
    return lax.dot_general(
        left, right, (((0,), (0,)), ((), ())), preferred_element_type=jnp.float32
    )


def by_features(left, right):
    return lax.dot_general(
        left, right, (((1,), (1,)), ((), ())), preferred_element_type=jnp.float32
    )


def exchange_kernel(
    sizes, pre_ref, og_ref, lin_ref, win_hbm, wout_ref,
    res_ref, gee_ref, hid_ref, up_ref, lx_ref,
    win_ref, preb, bp, bq, part, rsp, red, rsz, full,
    load_sem, send_sem, recv_sem,
):
    levels, tok, per = sizes
    rows = tok // CHUNKS
    plane = 4
    s = lax.axis_index("section")
    dp = lax.axis_index("dp")
    m = lax.axis_index("mp")
    z = dp // 2
    y = dp % 2
    p = s * 2 + y

    def at_plane(d):
        s2 = (s + d // 2) % 2
        y2 = (y + d % 2) % 2
        return (s2, z * 2 + y2, m), s2 * 2 + y2

    def at_level(e):
        z2 = (z + e) % levels
        return (s, z2 * 2 + y, m), z2

    load = pltpu.make_async_copy(win_hbm, win_ref, load_sem)
    load.start()

    peers = [at_plane(d)[0] for d in range(1, plane)]
    peers += [at_level(e)[0] for e in range(1, levels)]
    other_core = (s, dp, (m + 1) % 2)
    peers.append(other_core)
    barrier = pltpu.get_barrier_semaphore()
    for peer in peers:
        pl.semaphore_signal(barrier, inc=1, device_id=peer, device_id_type=MESH)
    pl.semaphore_wait(barrier, len(peers))

    started = []

    def send(src, dst, device):
        spot = len(started)
        copy = pltpu.make_async_remote_copy(
            src_ref=src, dst_ref=dst, send_sem=send_sem.at[spot],
            recv_sem=recv_sem.at[spot], device_id=device, device_id_type=MESH,
        )
        copy.start()
        started.append(copy)
        return copy

    x_peer = at_plane(2)[0]
    away = pl.ds(pl.multiple_of((1 - s) * per, per), per)
    mine = pl.ds(pl.multiple_of(s * per, per), per)
    span = [slice(c * rows, (c + 1) * rows) for c in range(CHUNKS)]

    pre_in = [send(pre_ref.at[0, span[c], away], preb.at[c], x_peer) for c in range(CHUNKS)]
    waiting = {}
    piece = tok // PIECES
    pieces = []

    def send_piece():
        i = len(pieces)
        if i < PIECES:
            there = pl.ds(i * piece, piece)
            pieces.append(send(lin_ref.at[0, there, :], lx_ref.at[there, :], x_peer))

    def back(a, c, upper):
        value = by_features(upper, wout_ref[...])
        bp[a, c] = value.astype(jnp.bfloat16)
        waiting[a, c] = [send(bp.at[a, c], bq.at[a, c], other_core)]

    def arrived(a, c):
        for copy in waiting[a, c]:
            copy.wait_recv()

    def hidden_grad(a, c):
        if a == 0:
            pre_in[c].wait_recv()
            if c == 0:
                load.wait()
        arrived(a, c)
        layer = 1 - a
        own = pre_ref[0, span[c], mine]
        saved = jnp.where(s == layer, own, preb[c]).astype(jnp.float32)
        cdf = gelu_cdf(saved)
        total = bp[a, c].astype(jnp.float32) + bq[a, c].astype(jnp.float32)
        gee = (total * slope_from(saved, cdf)).astype(jnp.bfloat16)
        copies = []
        for d in (3, 2, 1, 0):
            device, spot = at_plane(d)
            width = part.shape[-1]
            cols = pl.ds(pl.multiple_of(spot * width, width), width)
            value = jnp.dot(gee, win_ref[:, cols], preferred_element_type=jnp.float32)
            part[a, c, d] = value.astype(jnp.bfloat16)
            if d:
                copies.append(send(part.at[a, c, d], rsp.at[a, c, d], device))
        waiting[a, c] = copies
        gee_ref[(layer + s) % 2, span[c], :] = gee
        hid_ref[a, span[c], :] = (saved * cdf).astype(jnp.bfloat16)

    def reduce_plane(a, c):
        arrived(a, c)
        total = part[a, c, 0].astype(jnp.float32)
        for d in range(1, plane):
            total = total + rsp[a, c, d].astype(jnp.float32)
        total = total.astype(jnp.bfloat16)
        for i in range(levels):
            red[a, c, i] = total[:, i * LANES:(i + 1) * LANES]
        copies = []
        for e in range(1, levels):
            device, spot = at_level(e)
            copies.append(send(red.at[a, c, spot], rsz.at[a, c, e], device))
        waiting[a, c] = copies
        send_piece()

    def reduce_level(a, c):
        arrived(a, c)
        if a == 0:
            cols = pl.ds(pl.multiple_of((p * levels + z) * LANES, LANES), LANES)
            total = og_ref[span[c], cols].astype(jnp.float32)
        else:
            total = full[0, c, p, z].astype(jnp.float32)
        total = total + red[a, c, z].astype(jnp.float32)
        for e in range(1, levels):
            total = total + rsz[a, c, e].astype(jnp.float32)
        full[a, c, p, z] = total.astype(jnp.bfloat16)
        here = full.at[a, c, p, z]
        waiting[a, c] = [send(here, here, at_level(e)[0]) for e in range(1, levels)]
        send_piece()

    def gather_plane(a, c):
        arrived(a, c)
        here = full.at[a, c, p]
        waiting[a, c] = [send(here, here, at_plane(d)[0]) for d in (3, 2, 1)]

    def finish(a, c):
        arrived(a, c)
        value = jnp.concatenate(
            [full[a, c, i, j] for i in range(plane) for j in range(levels)], axis=1
        )
        if a == 0:
            up_ref[span[c], :] = value
            back(1, c, value)
        else:
            res_ref[0, span[c], :] = jnp.where(s == 0, value, up_ref[span[c], :])

    for c in range(CHUNKS):
        back(0, c, og_ref[span[c], :])
    for a in range(2):
        for stage in (hidden_grad, reduce_plane, reduce_level, gather_plane, finish):
            for c in range(CHUNKS):
                stage(a, c)
    while len(pieces) < PIECES:
        send_piece()
    for copy in pieces:
        copy.wait_recv()
    for copy in started:
        copy.wait_send()


def grads_kernel(gee_ref, hid_ref, lin_ref, lx_ref, og_ref, up_ref, gin_ref, gout_ref):
    def term(left, right):
        return by_tokens(left, right).astype(jnp.bfloat16).astype(jnp.float32)

    gin_ref[0, 0] = term(gee_ref[0], lin_ref[0]) + term(gee_ref[1], lx_ref[...])
    gout_ref[0, 0] = term(hid_ref[0], og_ref[...]) + term(hid_ref[1], up_ref[...])


def fused_body(layer_inputs, pre_act, out_grad, w_in, w_out):
    tok, width = out_grad.shape
    per = w_in.shape[2]
    levels = lax.axis_size("dp") // 2
    rows = tok // CHUNKS
    bf = jnp.bfloat16
    slots = 4 + 0 * levels
    copies = CHUNKS * (3 + 2 * (6 + 2 * (levels - 1))) + PIECES
    vmem = pl.BlockSpec(memory_space=pltpu.VMEM)
    anyw = pl.BlockSpec(memory_space=pl.ANY)
    result, gees, hids, upper, other_in = pl.pallas_call(
        functools.partial(exchange_kernel, (levels, tok, per)),
        out_shape=(
            jax.ShapeDtypeStruct((1, tok, width), bf),
            jax.ShapeDtypeStruct((2, tok, per), bf),
            jax.ShapeDtypeStruct((2, tok, per), bf),
            jax.ShapeDtypeStruct((tok, width), bf),
            jax.ShapeDtypeStruct((tok, width), bf),
        ),
        in_specs=[vmem, vmem, anyw, anyw, vmem],
        out_specs=(vmem, vmem, vmem, vmem, anyw),
        scratch_shapes=[
            pltpu.VMEM((per, width), bf),
            pltpu.VMEM((CHUNKS, rows, per), bf),
            pltpu.VMEM((2, CHUNKS, rows, per), bf),
            pltpu.VMEM((2, CHUNKS, rows, per), bf),
            pltpu.VMEM((2, CHUNKS, slots, rows, width // 4), bf),
            pltpu.VMEM((2, CHUNKS, slots, rows, width // 4), bf),
            pltpu.VMEM((2, CHUNKS, levels, rows, LANES), bf),
            pltpu.VMEM((2, CHUNKS, levels, rows, LANES), bf),
            pltpu.VMEM((2, CHUNKS, 4, levels, rows, LANES), bf),
            pltpu.SemaphoreType.DMA,
            pltpu.SemaphoreType.DMA((copies,)),
            pltpu.SemaphoreType.DMA((copies,)),
        ],
        compiler_params=pltpu.CompilerParams(
            collective_id=0, has_side_effects=True, vmem_limit_bytes=VMEM_BYTES
        ),
    )(pre_act, out_grad, layer_inputs, w_in.reshape(per, width), w_out.reshape(per, width))
    tile = min(512, width)
    whole = pl.BlockSpec((2, tok, per), lambda j: (0, 0, 0))
    cols = pl.BlockSpec((tok, tile), lambda j: (0, j))
    grad = pl.BlockSpec((1, 1, per, tile), lambda j: (0, 0, 0, j))
    shape = jax.ShapeDtypeStruct((1, 1, per, width), jnp.float32)
    grad_in, grad_out = pl.pallas_call(
        grads_kernel,
        grid=(width // tile,),
        out_shape=(shape, shape),
        in_specs=[
            whole, whole, pl.BlockSpec((1, tok, tile), lambda j: (0, 0, j)), cols, cols, cols,
        ],
        out_specs=(grad, grad),
    )(gees, hids, layer_inputs, other_in, out_grad, upper)
    return result, grad_in, grad_out


def plain_body(layer_inputs, pre_act, out_grad, w_in, w_out):
    sections = lax.axis_size("section")
    spot = lax.axis_index("section")
    tok, width = out_grad.shape
    per = w_in.shape[2]
    in_rows = w_in.reshape(per, width)
    out_rows = w_out.reshape(per, width)
    blocks = pre_act.reshape(tok, sections, per)
    saved_all = lax.all_to_all(blocks, "section", split_axis=1, concat_axis=0, tiled=True)
    saved_all = saved_all.reshape(sections, tok, per).astype(jnp.float32)
    inputs = lax.all_gather(layer_inputs, "section", axis=0, tiled=True)
    upper = out_grad
    grad_in = jnp.zeros((per, width), jnp.float32)
    grad_out = jnp.zeros((per, width), jnp.float32)
    results = []
    for layer in reversed(range(sections)):
        partial_value = by_features(upper, out_rows).astype(jnp.bfloat16)
        total = lax.psum(partial_value.astype(jnp.float32), "mp")
        saved = saved_all[layer]
        cdf = gelu_cdf(saved)
        gee = (total * slope_from(saved, cdf)).astype(jnp.bfloat16)
        hidden = (saved * cdf).astype(jnp.bfloat16)
        branch = jnp.dot(gee, in_rows, preferred_element_type=jnp.float32)
        branch = lax.psum(branch, ("section", "dp"))
        result = (upper.astype(jnp.float32) + branch).astype(jnp.bfloat16)
        grad_in = grad_in + rounded(by_tokens(gee, inputs[layer]))
        grad_out = grad_out + rounded(by_tokens(hidden, upper))
        results.append(result)
        upper = result
    mine = lax.dynamic_index_in_dim(jnp.stack(results[::-1]), spot, 0, keepdims=True)
    shape = (1, 1, per, width)
    return mine, grad_in.reshape(shape), grad_out.reshape(shape)


def body(layer_inputs, pre_act, out_grad, w_in, w_out):
    tok, width = out_grad.shape
    per = w_in.shape[2]
    groups = lax.axis_size("dp")
    suits = (
        lax.axis_size("section") == 2
        and lax.axis_size("mp") == 2
        and groups % 2 == 0
        and groups > 2
        and width == 2 * groups * LANES
        and per % LANES == 0
        and tok % (CHUNKS * 16) == 0
        and tok % (PIECES * 16) == 0
    )
    chosen = fused_body if suits else plain_body
    return chosen(layer_inputs, pre_act, out_grad, w_in, w_out)


def solution(mesh):
    in_specs = (
        P("section", None, "mp"),
        P("section", None, "dp"),
        P(None, "mp"),
        P("dp", "section", None, "mp"),
        P("dp", "section", None, "mp"),
    )
    out_specs = (
        P("section", None, "mp"),
        P("dp", "section", None, "mp"),
        P("dp", "section", None, "mp"),
    )
    return jax.shard_map(body, mesh=mesh, in_specs=in_specs, out_specs=out_specs, check_vma=False)
```

time: 510 us -> 62.5 us (0.12)
  waiting for transfers between devices: 428 us -> 0 us
  Pallas kernels: 0 us -> 59.7 us
  matrix products: 31.4 us -> 0 us
  blocking collectives: 20.7 us -> 0 us
  between operations: 14.2 us -> 0.64 us
  other arithmetic: 10.8 us -> 0 us
    psum x6 -> x0, waiting for transfers between devices: 268 us -> none  [the longest x3 217 us: advance(): total = lax.psum(branch.astype(jnp.bfloat16), 'dp').astype(jnp.float32)]
    all_gather x4 -> x0, waiting for transfers between devices: 138 us -> none  [the longest x1 60.3 us: body(): lax.all_gather(w_out, 'section', axis=1, tiled=True)]
    pallas_call x0 -> x2, Pallas kernels: none -> 59.7 us  [the longest x1 53.3 us: fused_body(): pl.pallas_call(functools.partial(exchange_kernel, (levels, tok, per)), ou...]
    dot_general x10 -> x0, matrix products: 31.4 us -> none  [the longest x3 12.7 us: advance(): lax.dot_general(upper, out_rows, (((1,), (1,)), ((), ())), preferred_elem...]
    all_gather x2 -> x0, blocking collectives: 20.7 us -> none  [the longest x1 12.7 us: body(): lax.all_gather(gees[None], 'section', axis=0, tiled=True)]
    ppermute x3 -> x0, waiting for transfers between devices: 20.4 us -> none  [shifted(): return lax.ppermute(value, axis, pairs)]
    reshape x2 -> x0, other arithmetic: 5.63 us -> none  [the longest x1 2.82 us: body(): grad_in = acc_in.reshape(1, 1, per_block, width)]
  transfers between devices with their start and end apart: 13 -> 0, of which waited for: 13 -> 0; matrix products, arithmetic and copies ran while one was open for 2% -> 0% of each run, Pallas kernels for 0% -> 0%
where the time goes in v1:
time: 62.5 us; the launch traced here: 62.2 us
  Pallas kernels  59.7 us (96%)
  local copies, waits for them, and re-layouts  1.88 us (3%)
  between operations  0.64 us (1%)
    pallas_call x1, Pallas kernels, fused_body(): pl.pallas_call(functools.partial(exchange_kernel, (levels, tok, per)), ou...  53.3 us
    pallas_call x1, Pallas kernels, fused_body(): pl.pallas_call(grads_kernel, grid=(width // tile,), out_shape=(shape, sha...  6.39 us
    unnamed x1, local copies, waits for them, and re-layouts  1.88 us

profile of v1, /device:TPU:0, one launch (start us, length us, event | category | flops | bytes accessed | tf_op | source)
XLA Modules:
  0.0 62.2 jit_solution(15167574274065828198)
XLA Ops:
  0.6 53.3 %shard_map.76 = (bf16[1,128,2048]{2,1,0:T(8,128)(2,1)}, bf16[2,128,512]{2,1,0:T(8,128)(2,1)}, bf16[2,128,512]{2,1,0:T(8,128)(2,1)}, bf16[128,2048]{1,0:T(8,128)(2,1)}, bf16[128,2048]{1,0:T(8,128)(2,1)}) custom-call(bf16[1,128,1024]{2,1,0:T(8,128)(2,1)} %pre_ref.1, bf16[128,2048]{1,0:T(8,128)(2,1)} %og_ref.3, bf16[1,128,2048]{2,1,0:T(8,128)(2,1)} %lin_ref.3, ...), custom_call_target="tpu_custom_call" | custom-call | tf_op jit(solution)/shard_map/pallas_call | solution.py:219
  54.0 6.4 %shard_map.77 = (f32[1,1,512,2048]{3,2,1,0:T(8,128)}, f32[1,1,512,2048]{3,2,1,0:T(8,128)}) custom-call(bf16[2,128,512]{2,1,0:T(8,128)(2,1)} %get-tuple-element.11.gee_ref, bf16[2,128,512]{2,1,0:T(8,128)(2,1)} %get-tuple-element.12.hid_ref, bf16[1,128,2048]{2,1,0:T(8,128)(2,1)} %lin_ref.3, bf16[128,2048]{1,0:T(8,128)(2,1)} %get-tuple-element.13.lx_ref, ...), custom_call_target="tpu_custom_call" | custom-call | tf_op jit(solution)/shard_map/pallas_call | solution.py:253
  60.4 1.9 %copy.9 = bf16[1,128,2048]{2,1,0:T(8,128)(2,1)} copy(bf16[1,128,2048]{2,1,0:T(8,128)(2,1)} %get-tuple-element.20) | data formatting | bytes 1048576

commit v2 on v1

--- a/solution.py
+++ b/solution.py
@@ -9,8 +9,9 @@
 
 MESH = pl.DeviceIdType.MESH
 CHUNKS = 2
-PIECES = 8
+PIECES = CHUNKS
 LANES = 128
+GRAD_TILE = 512
 VMEM_BYTES = 60 * 1024 * 1024
 
 
@@ -40,10 +41,11 @@
 
 
 def exchange_kernel(
-    sizes, pre_ref, og_ref, lin_ref, win_hbm, wout_ref,
-    res_ref, gee_ref, hid_ref, up_ref, lx_ref,
-    win_ref, preb, bp, bq, part, rsp, red, rsz, full,
-    load_sem, send_sem, recv_sem,
+    sizes, pre_hbm, og_hbm, lin_ref, win_hbm, wout_hbm,
+    res_hbm, gee_hbm, hid_hbm, up_hbm, lx_ref,
+    res_ref, gee_ref, hid_ref, up_ref, gee_turned, hid_turned,
+    pre_ref, og_ref, win_ref, wout_ref, preb, bp, bq, part, rsp, red, rsz, full,
+    load_sem, store_sem, send_sem, recv_sem,
 ):
     levels, tok, per = sizes
     rows = tok // CHUNKS
@@ -64,9 +66,6 @@
         z2 = (z + e) % levels
         return (s, z2 * 2 + y, m), z2
 
-    load = pltpu.make_async_copy(win_hbm, win_ref, load_sem)
-    load.start()
-
     peers = [at_plane(d)[0] for d in range(1, plane)]
     peers += [at_level(e)[0] for e in range(1, levels)]
     other_core = (s, dp, (m + 1) % 2)
@@ -74,9 +73,21 @@
     barrier = pltpu.get_barrier_semaphore()
     for peer in peers:
         pl.semaphore_signal(barrier, inc=1, device_id=peer, device_id_type=MESH)
-    pl.semaphore_wait(barrier, len(peers))
+
+    pairs = ((og_hbm, og_ref), (wout_hbm, wout_ref), (pre_hbm, pre_ref), (win_hbm, win_ref))
+    loads = [
+        pltpu.make_async_copy(src, dst, load_sem.at[i]) for i, (src, dst) in enumerate(pairs)
+    ]
+    for load in loads:
+        load.start()
 
     started = []
+    stores = []
+
+    def store(src, dst):
+        copy = pltpu.make_async_copy(src, dst, store_sem.at[len(stores)])
+        copy.start()
+        stores.append(copy)
 
     def send(src, dst, device):
         spot = len(started)
@@ -92,21 +103,27 @@
     away = pl.ds(pl.multiple_of((1 - s) * per, per), per)
     mine = pl.ds(pl.multiple_of(s * per, per), per)
     span = [slice(c * rows, (c + 1) * rows) for c in range(CHUNKS)]
-
-    pre_in = [send(pre_ref.at[0, span[c], away], preb.at[c], x_peer) for c in range(CHUNKS)]
     waiting = {}
-    piece = tok // PIECES
+    piece = tok // (PIECES * levels)
     pieces = []
-
-    def send_piece():
-        i = len(pieces)
-        if i < PIECES:
-            there = pl.ds(i * piece, piece)
-            pieces.append(send(lin_ref.at[0, there, :], lx_ref.at[there, :], x_peer))
-
-    def back(a, c, upper):
-        value = by_features(upper, wout_ref[...])
-        bp[a, c] = value.astype(jnp.bfloat16)
+    relays = []
+
+    def send_piece(a):
+        i = len(pieces) if a == 0 else len(relays)
+        if i >= PIECES:
+            return
+        begin = pl.multiple_of((z * PIECES + i) * piece, piece)
+        there = lx_ref.at[pl.ds(begin, piece), :]
+        if a == 0:
+            pieces.append(send(lin_ref.at[0, pl.ds(begin, piece), :], there, x_peer))
+        else:
+            pieces[i].wait_recv()
+            relays.append([send(there, there, at_level(e)[0]) for e in range(1, levels)])
+
+    def multiply(a, c, upper):
+        bp[a, c] = by_features(upper, wout_ref[...]).astype(jnp.bfloat16)
+
+    def back(a, c):
         waiting[a, c] = [send(bp.at[a, c], bq.at[a, c], other_core)]
 
     def arrived(a, c):
@@ -117,7 +134,7 @@
         if a == 0:
             pre_in[c].wait_recv()
             if c == 0:
-                load.wait()
+                loads[3].wait()
         arrived(a, c)
         layer = 1 - a
         own = pre_ref[0, span[c], mine]
@@ -135,8 +152,9 @@
             if d:
                 copies.append(send(part.at[a, c, d], rsp.at[a, c, d], device))
         waiting[a, c] = copies
-        gee_ref[(layer + s) % 2, span[c], :] = gee
-        hid_ref[a, span[c], :] = (saved * cdf).astype(jnp.bfloat16)
+        place = pl.multiple_of(((layer + s) % 2) * tok + c * rows, rows)
+        gee_ref[pl.ds(place, rows), :] = gee
+        hid_ref[pl.ds(a * tok + c * rows, rows), :] = (saved * cdf).astype(jnp.bfloat16)
 
     def reduce_plane(a, c):
         arrived(a, c)
@@ -151,7 +169,11 @@
             device, spot = at_level(e)
             copies.append(send(red.at[a, c, spot], rsz.at[a, c, e], device))
         waiting[a, c] = copies
-        send_piece()
+        if a == 1 and c == CHUNKS - 1:
+            gee_turned[...] = gee_ref[...].T
+            store(gee_turned, gee_hbm)
+            hid_turned[...] = hid_ref[...].T
+            store(hid_turned, hid_hbm)
 
     def reduce_level(a, c):
         arrived(a, c)
@@ -166,7 +188,8 @@
         full[a, c, p, z] = total.astype(jnp.bfloat16)
         here = full.at[a, c, p, z]
         waiting[a, c] = [send(here, here, at_level(e)[0]) for e in range(1, levels)]
-        send_piece()
+        if a == 0:
+            send_piece(0)
 
     def gather_plane(a, c):
         arrived(a, c)
@@ -180,30 +203,75 @@
         )
         if a == 0:
             up_ref[span[c], :] = value
-            back(1, c, value)
+            multiply(1, c, value)
+            back(1, c)
+            store(up_ref.at[span[c]], up_hbm.at[span[c]])
+            send_piece(1)
         else:
-            res_ref[0, span[c], :] = jnp.where(s == 0, value, up_ref[span[c], :])
-
-    for c in range(CHUNKS):
-        back(0, c, og_ref[span[c], :])
+            res_ref[span[c], :] = jnp.where(s == 0, value, up_ref[span[c], :])
+            store(res_ref.at[span[c]], res_hbm.at[span[c]])
+
+    loads[0].wait()
+    loads[1].wait()
+    multiply(0, 0, og_ref[span[0], :])
+    loads[2].wait()
+    pl.semaphore_wait(barrier, len(peers))
+    pre_in = [send(pre_ref.at[0, span[c], away], preb.at[c], x_peer) for c in range(CHUNKS)]
+    back(0, 0)
+    for c in range(1, CHUNKS):
+        multiply(0, c, og_ref[span[c], :])
+        back(0, c)
     for a in range(2):
         for stage in (hidden_grad, reduce_plane, reduce_level, gather_plane, finish):
             for c in range(CHUNKS):
                 stage(a, c)
-    while len(pieces) < PIECES:
-        send_piece()
-    for copy in pieces:
-        copy.wait_recv()
+    for copies in relays:
+        for copy in copies:
+            copy.wait_recv()
     for copy in started:
         copy.wait_send()
-
-
-def grads_kernel(gee_ref, hid_ref, lin_ref, lx_ref, og_ref, up_ref, gin_ref, gout_ref):
-    def term(left, right):
-        return by_tokens(left, right).astype(jnp.bfloat16).astype(jnp.float32)
-
-    gin_ref[0, 0] = term(gee_ref[0], lin_ref[0]) + term(gee_ref[1], lx_ref[...])
-    gout_ref[0, 0] = term(hid_ref[0], og_ref[...]) + term(hid_ref[1], up_ref[...])
+    for copy in stores:
+        copy.wait()
+
+
+def grads_kernel(
+    gee_hbm, hid_hbm, lin_hbm, lx_hbm, og_hbm, up_hbm, given_hbm,
+    res_hbm, gin_hbm, gout_hbm,
+    gee, hid, inputs, uppers, given, gin, gout, load_sem, store_sem,
+):
+    tok, width = og_hbm.shape
+    tile = min(GRAD_TILE, width)
+    pairs = (
+        (hid_hbm, hid), (og_hbm, uppers.at[:tok]), (up_hbm, uppers.at[tok:]),
+        (gee_hbm, gee), (lin_hbm.at[0], inputs.at[:tok]), (lx_hbm, inputs.at[tok:]),
+        (given_hbm, given),
+    )
+    loads = [
+        pltpu.make_async_copy(src, dst, load_sem.at[i]) for i, (src, dst) in enumerate(pairs)
+    ]
+    for load in loads:
+        load.start()
+    stores = []
+
+    def store(src, dst):
+        copy = pltpu.make_async_copy(src, dst, store_sem.at[len(stores)])
+        copy.start()
+        stores.append(copy)
+
+    sides = ((0, hid, uppers, gout, gout_hbm), (3, gee, inputs, gin, gin_hbm))
+    for first, left, right, held, out in sides:
+        for load in loads[first:first + 3]:
+            load.wait()
+        for t in range(width // tile):
+            cols = slice(t * tile, (t + 1) * tile)
+            held[:, cols] = jnp.dot(
+                left[...], right[:, cols], preferred_element_type=jnp.float32
+            )
+            store(held.at[:, cols], out.at[0, 0, :, cols])
+    loads[6].wait()
+    store(given, res_hbm.at[0])
+    for copy in stores:
+        copy.wait()
 
 
 def fused_body(layer_inputs, pre_act, out_grad, w_in, w_out):
@@ -212,32 +280,40 @@
     levels = lax.axis_size("dp") // 2
     rows = tok // CHUNKS
     bf = jnp.bfloat16
-    slots = 4 + 0 * levels
-    copies = CHUNKS * (3 + 2 * (6 + 2 * (levels - 1))) + PIECES
-    vmem = pl.BlockSpec(memory_space=pltpu.VMEM)
+    copies = CHUNKS * (3 + 2 * (6 + 2 * (levels - 1))) + PIECES * levels
     anyw = pl.BlockSpec(memory_space=pl.ANY)
     result, gees, hids, upper, other_in = pl.pallas_call(
         functools.partial(exchange_kernel, (levels, tok, per)),
         out_shape=(
-            jax.ShapeDtypeStruct((1, tok, width), bf),
-            jax.ShapeDtypeStruct((2, tok, per), bf),
-            jax.ShapeDtypeStruct((2, tok, per), bf),
+            jax.ShapeDtypeStruct((tok, width), bf),
+            jax.ShapeDtypeStruct((per, 2 * tok), bf),
+            jax.ShapeDtypeStruct((per, 2 * tok), bf),
             jax.ShapeDtypeStruct((tok, width), bf),
             jax.ShapeDtypeStruct((tok, width), bf),
         ),
-        in_specs=[vmem, vmem, anyw, anyw, vmem],
-        out_specs=(vmem, vmem, vmem, vmem, anyw),
+        in_specs=[anyw] * 5,
+        out_specs=[anyw] * 5,
         scratch_shapes=[
+            pltpu.VMEM((tok, width), bf),
+            pltpu.VMEM((2 * tok, per), bf),
+            pltpu.VMEM((2 * tok, per), bf),
+            pltpu.VMEM((tok, width), bf),
+            pltpu.VMEM((per, 2 * tok), bf),
+            pltpu.VMEM((per, 2 * tok), bf),
+            pltpu.VMEM(pre_act.shape, bf),
+            pltpu.VMEM((tok, width), bf),
+            pltpu.VMEM((per, width), bf),
             pltpu.VMEM((per, width), bf),
             pltpu.VMEM((CHUNKS, rows, per), bf),
             pltpu.VMEM((2, CHUNKS, rows, per), bf),
             pltpu.VMEM((2, CHUNKS, rows, per), bf),
-            pltpu.VMEM((2, CHUNKS, slots, rows, width // 4), bf),
-            pltpu.VMEM((2, CHUNKS, slots, rows, width // 4), bf),
+            pltpu.VMEM((2, CHUNKS, 4, rows, width // 4), bf),
+            pltpu.VMEM((2, CHUNKS, 4, rows, width // 4), bf),
             pltpu.VMEM((2, CHUNKS, levels, rows, LANES), bf),
             pltpu.VMEM((2, CHUNKS, levels, rows, LANES), bf),
             pltpu.VMEM((2, CHUNKS, 4, levels, rows, LANES), bf),
-            pltpu.SemaphoreType.DMA,
+            pltpu.SemaphoreType.DMA((4,)),
+            pltpu.SemaphoreType.DMA((2 * CHUNKS + 2,)),
             pltpu.SemaphoreType.DMA((copies,)),
             pltpu.SemaphoreType.DMA((copies,)),
         ],
@@ -245,21 +321,26 @@
             collective_id=0, has_side_effects=True, vmem_limit_bytes=VMEM_BYTES
         ),
     )(pre_act, out_grad, layer_inputs, w_in.reshape(per, width), w_out.reshape(per, width))
-    tile = min(512, width)
-    whole = pl.BlockSpec((2, tok, per), lambda j: (0, 0, 0))
-    cols = pl.BlockSpec((tok, tile), lambda j: (0, j))
-    grad = pl.BlockSpec((1, 1, per, tile), lambda j: (0, 0, 0, j))
+    tiles = width // min(GRAD_TILE, width)
     shape = jax.ShapeDtypeStruct((1, 1, per, width), jnp.float32)
-    grad_in, grad_out = pl.pallas_call(
+    return pl.pallas_call(
         grads_kernel,
-        grid=(width // tile,),
-        out_shape=(shape, shape),
-        in_specs=[
-            whole, whole, pl.BlockSpec((1, tok, tile), lambda j: (0, 0, j)), cols, cols, cols,
+        out_shape=(jax.ShapeDtypeStruct((1, tok, width), bf), shape, shape),
+        in_specs=[anyw] * 7,
+        out_specs=[anyw] * 3,
+        scratch_shapes=[
+            pltpu.VMEM((per, 2 * tok), bf),
+            pltpu.VMEM((per, 2 * tok), bf),
+            pltpu.VMEM((2 * tok, width), bf),
+            pltpu.VMEM((2 * tok, width), bf),
+            pltpu.VMEM((tok, width), bf),
+            pltpu.VMEM((per, width), jnp.float32),
+            pltpu.VMEM((per, width), jnp.float32),
+            pltpu.SemaphoreType.DMA((7,)),
+            pltpu.SemaphoreType.DMA((2 * tiles + 1,)),
         ],
-        out_specs=(grad, grad),
-    )(gees, hids, layer_inputs, other_in, out_grad, upper)
-    return result, grad_in, grad_out
+        compiler_params=pltpu.CompilerParams(vmem_limit_bytes=VMEM_BYTES),
+    )(gees, hids, layer_inputs, other_in, out_grad, upper, result)
 
 
 def plain_body(layer_inputs, pre_act, out_grad, w_in, w_out):
@@ -308,7 +389,7 @@
         and width == 2 * groups * LANES
         and per % LANES == 0
         and tok % (CHUNKS * 16) == 0
-        and tok % (PIECES * 16) == 0
+        and tok % (PIECES * groups * 8) == 0
     )
     chosen = fused_body if suits else plain_body
     return chosen(layer_inputs, pre_act, out_grad, w_in, w_out)

time: 62.5 us -> 57.1 us (0.914)
  Pallas kernels: 59.7 us -> 56.3 us
  local copies, waits for them, and re-layouts: 1.88 us -> 0 us
    pallas_call x1, Pallas kernels: 53.3 us -> 51.2 us  [fused_body(): pl.pallas_call(functools.partial(exchange_kernel, (levels, tok, per)), ou...]
    unnamed x1 -> x0, local copies, waits for them, and re-layouts: 1.88 us -> none
    pallas_call x1, Pallas kernels: 6.39 us -> 5.16 us  [fused_body(): pl.pallas_call(grads_kernel, out_shape=(jax.ShapeDtypeStruct((1, tok, wid...]
where the time goes in v2:
time: 57.1 us; the launch traced here: 57 us
  Pallas kernels  56.3 us (99%)
  between operations  0.64 us (1%)
    pallas_call x1, Pallas kernels, fused_body(): pl.pallas_call(functools.partial(exchange_kernel, (levels, tok, per)), ou...  51.2 us
    pallas_call x1, Pallas kernels, fused_body(): pl.pallas_call(grads_kernel, out_shape=(jax.ShapeDtypeStruct((1, tok, wid...  5.16 us

profile of v2, /device:TPU:0, one launch (start us, length us, event | category | flops | bytes accessed | tf_op | source)
XLA Modules:
  0.0 57.0 jit_solution(11282102140741005875)
XLA Ops:
  0.6 51.2 %shard_map.76 = (bf16[128,2048]{1,0:T(8,128)(2,1)}, bf16[512,256]{1,0:T(8,128)(2,1)}, bf16[512,256]{1,0:T(8,128)(2,1)}, bf16[128,2048]{1,0:T(8,128)(2,1)}, bf16[128,2048]{1,0:T(8,128)(2,1)}) custom-call(bf16[1,128,1024]{2,1,0:T(8,128)(2,1)} %pre_hbm.1, bf16[128,2048]{1,0:T(8,128)(2,1)} %og_hbm.3, bf16[1,128,2048]{2,1,0:T(8,128)(2,1)} %lin_hbm.1, ...), custom_call_target="tpu_custom_call" | custom-call | tf_op jit(solution)/shard_map/pallas_call | solution.py:285
  51.8 5.2 %shard_map.77 = (bf16[1,128,2048]{2,1,0:T(8,128)(2,1)}, f32[1,1,512,2048]{3,2,1,0:T(8,128)}, f32[1,1,512,2048]{3,2,1,0:T(8,128)}) custom-call(bf16[512,256]{1,0:T(8,128)(2,1)} %get-tuple-element.8.gee_hbm, bf16[512,256]{1,0:T(8,128)(2,1)} %get-tuple-element.9.hid_hbm, bf16[1,128,2048]{2,1,0:T(8,128)(2,1)} %lin_hbm.1, ...), custom_call_target="tpu_custom_call" | custom-call | tf_op jit(solution)/shard_map/pallas_call | solution.py:326
